TPU v7x, 512 devices: a whole 4x8x8 slice. The times are simulated.
512 devices in a mesh: mem: 32 (over z_hi, y, core), kvh: 4 (over z_lo), row: 4 (over x).
Axes of the slice: x: 4, y: 8, z: 8 (z_hi: 2, z_lo: 4; z = z_hi * 4 + z_lo), core: 2. Of those that a mesh axis runs over, the one named last changes fastest.
Arguments:
- queries: bfloat16 [1024, 8192], P(('mem', 'kvh', 'row')), may hold values from -120 to 120
- output_gradient: bfloat16 [1024, 8192], P(('mem', 'kvh', 'row')), may hold values from -6 to 6
- keys: bfloat16 [24576, 1024], P('mem', 'kvh'), may hold values from -6 to 6
- values: bfloat16 [24576, 1024], P('mem', 'kvh'), may hold values from -6 to 6
- text_video: int32 [128, 8], P(None, 'row'), may hold values from 0 to 95
- video_blocks: int32 [96], replicated, may hold values from 1 to 4, 192 in all
Outputs:
- attention_out: bfloat16 [1024, 8192], P(('mem', 'kvh', 'row'))
- query_grad: bfloat16 [1024, 8192], P(('mem', 'kvh', 'row'))
- keys_gradient: bfloat16 [24576, 1024], P('mem', 'kvh')
- values_gradient: bfloat16 [24576, 1024], P('mem', 'kvh')
Inputs may be any that keep to these rules, and one draw needn't show every extreme that they name: Row sees images 0 to text_video. `video_blocks`: they sum to 192.
All inputs are finite; a program needn't handle non-finite values.
Results may differ from a plain program's by a relative error of at most 0.015.
Values may be sent and summed in bfloat16 or wider, within the bound.
A program may use at most 64 MiB of HBM per device.

v0:
```python
import jax
import jax.numpy as jnp
from jax import lax
from jax.sharding import PartitionSpec as P

QUERY_HEADS = 64
KEY_VALUE_HEADS = 8
HEAD_WIDTH = 128
FRAME = 128
masked_score = -1e30


def in_one_piece(arrays, axis, dim, along):
    both = jnp.concatenate(arrays, axis=along)
    result, at, outs = (lax.all_gather(both, axis, axis=dim, tiled=True), 0, [])
    for a in arrays:
        outs.append(lax.slice_in_dim(result, at, at + a.shape[along], axis=along))
        at += a.shape[along]
    return tuple(outs)


def sent_to_all(array, axis):
    count = lax.axis_size(axis)
    return lax.all_to_all(
        jnp.broadcast_to(array[None], (count, *array.shape)), axis, 0, 0, tiled=True
    )


def of_everyone(array, axis):
    everything = sent_to_all(array, axis)
    return jnp.sum(everything.astype(jnp.float32), axis=0)


def cut_along(array, dim, count):
    before, after = (array.shape[:dim], array.shape[dim + 1 :])
    return jnp.moveaxis(array.reshape(*before, count, -1, *after), dim, 0)


def sent_and_summed(array, axis, dim):
    pieces = cut_along(array, dim, lax.axis_size(axis))
    arrived = lax.all_to_all(pieces, axis, split_axis=0, concat_axis=0, tiled=True)
    return arrived.astype(jnp.float32).sum(axis=0)


def video_of_block(video_blocks, first_block, block_count):
    block_ends = jnp.cumsum(video_blocks)
    blocks = first_block + jnp.arange(block_count, dtype=jnp.int32)
    return jnp.sum((block_ends[None, :] <= blocks[:, None]).astype(jnp.int32), axis=1)


def per_device(queries, output_gradient, keys, values, text_video, video_blocks):
    inverse_root = HEAD_WIDTH ** (-0.5)
    heads_per_group = QUERY_HEADS // KEY_VALUE_HEADS
    mem_count = lax.axis_size("mem")
    local_query, local_grad = (
        lax.all_to_all(queries, "kvh", split_axis=1, concat_axis=0, tiled=True),
        lax.all_to_all(output_gradient, "kvh", split_axis=1, concat_axis=0, tiled=True),
    )
    query_rows, grad_rows = in_one_piece((local_query, local_grad), "mem", 0, 1)
    group_size = query_rows.shape[0]
    own_count = local_query.shape[0]
    key_local = keys.shape[1] // HEAD_WIDTH
    frames = keys.shape[0] // FRAME
    query_four = query_rows.reshape(group_size, key_local, heads_per_group, HEAD_WIDTH)
    grad_four = grad_rows.reshape(group_size, key_local, heads_per_group, HEAD_WIDTH)
    key_frames = keys.reshape(frames, FRAME, key_local, HEAD_WIDTH)
    value_frames = values.reshape(frames, FRAME, key_local, HEAD_WIDTH)
    key_video = video_of_block(video_blocks, lax.axis_index("mem") * frames, frames)
    visible = key_video[None, :] <= text_video.reshape(group_size)[:, None]
    frame_ids = jnp.arange(frames, dtype=jnp.int32)

    def frame_scores(frame_index):
        key_block = lax.dynamic_index_in_dim(key_frames, frame_index, 0, keepdims=False)
        scores = (
            jnp.einsum("rghd,jgd->rghj", query_four, key_block, preferred_element_type=jnp.float32)
            * inverse_root
        )
        seen_rows = lax.dynamic_index_in_dim(visible, frame_index, 1, keepdims=False)[
            :, None, None, None
        ]
        return (jnp.where(seen_rows, scores, masked_score), seen_rows, key_block)

    def forward_step(running, frame_index):
        running_top, totals, numerator = running
        scores, seen_rows, key_block = frame_scores(frame_index)
        new_top = jnp.maximum(running_top, jnp.max(scores, axis=3))
        weight = jnp.where(seen_rows, jnp.exp(scores - new_top[..., None]), 0.0)
        shrink_factor = jnp.exp(running_top - new_top)
        totals = totals * shrink_factor + jnp.sum(weight, axis=3)
        value_block = lax.dynamic_index_in_dim(value_frames, frame_index, 0, keepdims=False)
        numerator = numerator * shrink_factor[..., None] + jnp.einsum(
            "rghj,jgd->rghd",
            weight.astype(jnp.bfloat16),
            value_block,
            preferred_element_type=jnp.float32,
        )
        return ((new_top, totals, numerator), None)

    stat_shape = (group_size, key_local, heads_per_group)
    start_state = (
        jnp.full(stat_shape, masked_score, jnp.float32),
        jnp.zeros(stat_shape, jnp.float32),
        jnp.zeros(stat_shape + (HEAD_WIDTH,), jnp.float32),
    )
    (local_top, local_totals, numerator), unused = lax.scan(forward_step, start_state, frame_ids)
    own_grad = local_grad.reshape(own_count, key_local, heads_per_group, HEAD_WIDTH).astype(
        jnp.float32
    )
    sent = (
        numerator.reshape((mem_count, own_count) + numerator.shape[1:]),
        local_top.reshape((mem_count, own_count) + stat_shape[1:]),
        local_totals.reshape((mem_count, own_count) + stat_shape[1:]),
    )
    numerator_src, top_src, totals_src = (
        lax.all_to_all(sent[0], "mem", split_axis=0, concat_axis=0, tiled=True),
        lax.all_to_all(sent[1], "mem", split_axis=0, concat_axis=0, tiled=True),
        lax.all_to_all(sent[2], "mem", split_axis=0, concat_axis=0, tiled=True),
    )
    own_top = jnp.max(top_src, axis=0)
    factor = jnp.exp(top_src - own_top)
    own_totals = jnp.sum(totals_src * factor, axis=0)
    attention = jnp.sum(numerator_src * factor[..., None], axis=0) / own_totals[..., None]
    delta_own = jnp.sum(own_grad * attention, axis=3)
    own_log = own_top + jnp.log(own_totals)
    log_mass, delta_rows = in_one_piece((own_log, delta_own), "mem", 0, 1)
    attention_low = attention.reshape(own_count, key_local * heads_per_group * HEAD_WIDTH).astype(
        jnp.bfloat16
    )

    def backward_step(query_grad, frame_index):
        scores, seen_rows, key_block = frame_scores(frame_index)
        value_block = lax.dynamic_index_in_dim(value_frames, frame_index, 0, keepdims=False)
        probability = jnp.where(seen_rows, jnp.exp(scores - log_mass[..., None]), 0.0)
        prob_grad = jnp.einsum(
            "rghd,jgd->rghj", grad_four, value_block, preferred_element_type=jnp.float32
        )
        score_grad = (probability * (prob_grad - delta_rows[..., None])).astype(jnp.bfloat16)
        query_grad = (
            query_grad
            + jnp.einsum(
                "rghj,jgd->rghd", score_grad, key_block, preferred_element_type=jnp.float32
            )
            * inverse_root
        )
        key_part = (
            jnp.einsum("rghj,rghd->jgd", score_grad, query_four, preferred_element_type=jnp.float32)
            * inverse_root
        )
        value_part = jnp.einsum(
            "rghj,rghd->jgd",
            probability.astype(jnp.bfloat16),
            grad_four,
            preferred_element_type=jnp.float32,
        )
        return (query_grad, (key_part, value_part))

    query_grad, (key_parts, value_parts) = lax.scan(
        backward_step, jnp.zeros(stat_shape + (HEAD_WIDTH,), jnp.float32), frame_ids
    )
    key_sum = key_parts.reshape(keys.shape)
    value_sum = value_parts.reshape(values.shape)
    key_sum, value_sum = (
        of_everyone(key_sum.astype(jnp.bfloat16), "row").astype(jnp.float32),
        of_everyone(value_sum.astype(jnp.bfloat16), "row").astype(jnp.float32),
    )
    own_query_grad = sent_and_summed(query_grad.astype(jnp.bfloat16), "mem", 0)
    query_low = own_query_grad.reshape(own_count, key_local * heads_per_group * HEAD_WIDTH).astype(
        jnp.bfloat16
    )
    attention_text, query_text = (
        lax.all_to_all(attention_low, "kvh", split_axis=0, concat_axis=1, tiled=True),
        lax.all_to_all(query_low, "kvh", split_axis=0, concat_axis=1, tiled=True),
    )
    return (
        attention_text,
        query_text,
        key_sum.astype(jnp.bfloat16),
        value_sum.astype(jnp.bfloat16),
    )


def solution(mesh):
    in_specs = (
        P(("mem", "kvh", "row"), None),
        P(("mem", "kvh", "row"), None),
        P("mem", "kvh"),
        P("mem", "kvh"),
        P(None, "row"),
        P(),
    )
    out_specs = (
        P(("mem", "kvh", "row"), None),
        P(("mem", "kvh", "row"), None),
        P("mem", "kvh"),
        P("mem", "kvh"),
    )
    return jax.shard_map(
        per_device, mesh=mesh, in_specs=in_specs, out_specs=out_specs, check_vma=False
    )
```

profile of v0, /device:TPU:8, one launch (start us, length us, event | category | flops | bytes accessed | tf_op | source)
XLA Modules:
  0.0 536.6 jit_solution(9227071309435036342)
XLA Ops:
  7.2 13.1 %all_to_all.100 = bf16[2,4,2048]{2,0,1:T(2,128)(2,1)S(1)} all-to-all(bf16[2,4,2048]{2,0,1:T(2,128)(2,1)} %bitcast.198), channel_id=1, replica_groups=mesh['mem'=32,'kvh'=4,'row'=4] {'kvh'}, dimensions={1} | all-to-all | bytes 65536 | tf_op jit(solution)/shard_map/all_to_all | solution.py:57
  20.3 3.3 all-to-all-start
  23.6 5.5 %all-to-all-done = bf16[2,4,2048]{2,0,1:T(2,128)(2,1)S(1)} async-done(((bf16[2,4,2048]{2,0,1:T(2,128)(2,1)}), bf16[2,4,2048]{2,0,1:T(2,128)(2,1)S(1)}, u32[]{:S(2)}, u32[]{:S(2)}) %all-to-all-start) | async-done | bytes 32800 | tf_op jit(solution)/shard_map/all_to_all | solution.py:56
  32.0 93.0 %all-gather.2.cloned.1.call-done = bf16[256,4096]{1,0:T(8,128)(2,1)} async-done(((bf16[8,4096]{1,0:T(8,128)(2,1)}), bf16[256,4096]{1,0:T(8,128)(2,1)}) %all-gather.2.cloned.1.call-update) | async-done | bytes 2097168 | tf_op jit(solution)/shard_map/all_gather | solution.py:15
  125.0 2.7 fusion.36
  129.6 50.9 %while.30 = (s32[]{:T(128)}, f32[256,2,8]{0,2,1:T(8,128)S(1)}, f32[256,2,8]{0,2,1:T(8,128)S(1)}, f32[256,2,8,128]{0,3,2,1:T(8,128)}, s32[6]{0:T(128)S(1)}, /*ind...) while((s32[]{:T(128)}, f32[256,2,8]{0,2,1:T(8,128)S(1)}, ...), condition=%wide.region_5.6_spmd.clone, body=%wide.region_2.5_spmd.clone.sunk | while | flops 276844544 | bytes 12191419 | solution.py:105
  141.8 3.7 bitcast_add_fusion.4
  150.6 3.7 bitcast_add_fusion.4
  159.3 3.7 bitcast_add_fusion.4
  168.1 3.7 bitcast_add_fusion.4
  176.8 3.7 bitcast_add_fusion.4
  183.3 5.6 %all-to-all-start.3 = ((f32[32,1,128]{2,1,0:T(1,128)}), f32[32,1,128]{2,1,0:T(1,128)S(1)}, u32[]{:S(2)}, u32[]{:S(2)}) async-start(f32[32,1,128]{2,1,0:T(1,128)} %reshape.134), calls=%async_computation.3 | async-start | bytes 32768 | tf_op jit(solution)/shard_map/all_to_all | solution.py:116
  191.7 8.3 %all-to-all-done.3 = f32[32,1,128]{2,1,0:T(1,128)S(1)} async-done(((f32[32,1,128]{2,1,0:T(1,128)}), f32[32,1,128]{2,1,0:T(1,128)S(1)}, u32[]{:S(2)}, u32[]{:S(2)}) %all-to-all-start.3) | async-done | bytes 16416 | tf_op jit(solution)/shard_map/all_to_all | solution.py:116
  200.0 4.9 all-to-all-start.4
  206.9 9.2 %all-to-all-done.4 = f32[32,1,128]{2,1,0:T(1,128)S(1)} async-done(((f32[32,1,128]{2,1,0:T(1,128)}), f32[32,1,128]{2,1,0:T(1,128)S(1)}, u32[]{:S(2)}, u32[]{:S(2)}) %all-to-all-start.4) | async-done | bytes 16416 | tf_op jit(solution)/shard_map/all_to_all | solution.py:117
  216.7 5.1 all-to-all-start.2
  228.7 50.4 %all-to-all-done.2 = f32[32,8,2,8,128]{4,3,2,1,0:T(8,128)S(1)} async-done(((f32[32,8,2,8,128]{4,3,2,1,0:T(8,128)}), f32[32,8,2,8,128]{4,3,2,1,0:T(8,128)S(1)}, u32[]{:S(2)}, u32[]{:S(2)}) %all-to-all-start.2) | async-done | bytes 2097184 | tf_op jit(solution)/shard_map/all_to_all | solution.py:115
  280.1 46.2 %all_gather.7 = f32[256,4,8]{2,1,0:T(4,128)S(1)} all-gather(f32[8,4,8]{2,1,0:T(4,128)S(1)} %copy.109), channel_id=1, replica_groups=mesh['mem'=32,'kvh'=4,'row'=4] {'mem'}, dimensions={0}, use_global_device_ids=true | all-gather | bytes 33792 | tf_op jit(solution)/shard_map/all_gather | solution.py:15
  327.3 3.9 all-to-all-start.5
  331.2 87.4 %while.31 = (s32[]{:T(128)}, f32[256,2,8,128]{0,3,2,1:T(8,128)}, bf16[6,128,2,128]{3,1,2,0:T(8,128)(2,1)}, bf16[6,128,2,128]{3,1,2,0:T(8,128)(2,1)}, s32[6]{0:T(...) while((s32[]{:T(128)}, f32[256,2,8,128]{0,3,2,1:T(8,128)}, ...), condition=%wide.region_11.12_spmd.clone, body=%wide.region_10.11_spmd.clone.sunk | while | flops 676888576 | bytes 22776864 | solution.py:157
  352.4 3.4 bitcast_add_fusion.5
  367.2 3.4 bitcast_add_fusion.5
  382.0 3.4 bitcast_add_fusion.5
  396.8 3.4 bitcast_add_fusion.5
  411.7 3.4 bitcast_add_fusion.5
  421.4 4.5 all-to-all-start.8
  427.8 19.5 %all-to-all-done.8 = bf16[4,768,256]{2,1,0:T(8,128)(2,1)} async-done(((bf16[4,768,256]{2,1,0:T(8,128)(2,1)}), bf16[4,768,256]{2,1,0:T(8,128)(2,1)}, u32[]{:S(2)}, u32[]{:S(2)}) %all-to-all-start.8) | async-done | bytes 1572896 | tf_op jit(solution)/shard_map/all_to_all | solution.py:24
  447.3 12.5 %all-to-all-start.6 = ((bf16[32,8,2,8,128]{4,3,2,1,0:T(8,128)(2,1)}), bf16[32,8,2,8,128]{4,3,2,1,0:T(8,128)(2,1)S(1)}, u32[]{:S(2)}, u32[]{:S(2)}) async-start(bf16[32,8,2,8,128]{4,3,2,1,0:T(8,128)(2,1)} %bitcast.10), calls=%async_computation.6 | async-start | bytes 2097152 | tf_op jit(solution)/shard_map/all_to_all | solution.py:41
  461.2 31.6 %all-to-all-done.6 = bf16[32,8,2,8,128]{4,3,2,1,0:T(8,128)(2,1)S(1)} async-done(((bf16[32,8,2,8,128]{4,3,2,1,0:T(8,128)(2,1)}), bf16[32,8,2,8,128]{4,3,2,1,0:T(8,128)(2,1)S(1)}, u32[]{:S(2)}, u32[]{:S(2)}) %all-to-all-start.6) | async-done | bytes 1048608 | tf_op jit(solution)/shard_map/all_to_all | solution.py:41
  494.1 3.6 all-to-all-start.9
  498.5 18.8 %all-to-all-done.9 = bf16[4,768,256]{2,1,0:T(8,128)(2,1)S(1)} async-done(((bf16[4,768,256]{2,1,0:T(8,128)(2,1)}), bf16[4,768,256]{2,1,0:T(8,128)(2,1)S(1)}, u32[]{:S(2)}, u32[]{:S(2)}) %all-to-all-start.9) | async-done | bytes 1572896 | tf_op jit(solution)/shard_map/all_to_all | solution.py:24
  517.2 4.8 all-to-all-start.7
  (247 shorter events, 115.0 us)
Async XLA Ops:
  7.2 23.9 %copy-start.4 = (bf16[768,256]{1,0:T(8,128)(2,1)S(1)}, bf16[768,256]{1,0:T(8,128)(2,1)}, u32[]{:S(2)}) copy-start(bf16[768,256]{1,0:T(8,128)(2,1)} %param.13) | copy-start | bytes 1179652
  7.2 24.0 %copy-start.11 = (s32[96]{0:T(128)S(1)}, s32[96]{0:T(128)}, u32[]{:S(2)}) copy-start(s32[96]{0:T(128)} %param.15) | copy-start | bytes 1156
  7.2 24.3 %copy-start.10 = (s32[128,2]{0,1:T(2,128)S(1)}, s32[128,2]{0,1:T(2,128)}, u32[]{:S(2)}) copy-start(s32[128,2]{0,1:T(2,128)} %param.14) | copy-start | bytes 3076
  20.3 8.9 %all-to-all-start = ((bf16[2,4,2048]{2,0,1:T(2,128)(2,1)}), bf16[2,4,2048]{2,0,1:T(2,128)(2,1)S(1)}, u32[]{:S(2)}, u32[]{:S(2)}) async-start(bf16[2,4,2048]{2,0,1:T(2,128)(2,1)} %bitcast.199), calls=%async_computation | async-start | bytes 65536 | tf_op jit(solution)/shard_map/all_to_all | solution.py:56
  23.5 101.5 %all-gather.2.cloned.1.call-start = ((), (), s32[]{:S(2)}) async-start(), calls=%async_computation.10 | async-start | bytes 2162688 | tf_op jit(solution)/shard_map/all_gather | solution.py:15
  180.6 26.4 %copy-start.3 = (bf16[6,128,2,128]{3,2,1,0:T(2,128)(2,1)}, bf16[6,128,2,128]{3,2,1,0:T(2,128)(2,1)S(1)}, u32[]{:S(2)}) copy-start(bf16[6,128,2,128]{3,2,1,0:T(2,128)(2,1)S(1)} %get-tuple-element.573) | copy-start | bytes 1179652
  180.6 26.4 %copy-start.6 = (pred[256,6]{0,1:T(8,128)(4,1)}, pred[256,6]{0,1:T(8,128)(4,1)S(1)}, u32[]{:S(2)}) copy-start(pred[256,6]{0,1:T(8,128)(4,1)S(1)} %get-tuple-element.579) | copy-start | bytes 4612
  180.6 24.4 %copy-start.2 = (f32[256,2,8,128]{0,3,2,1:T(8,128)S(1)}, f32[256,2,8,128]{0,3,2,1:T(8,128)}, u32[]{:S(2)}) copy-start(f32[256,2,8,128]{0,3,2,1:T(8,128)} %get-tuple-element.117) | copy-start | bytes 6291460
  183.3 16.7 %all-to-all-start.3 = ((f32[32,1,128]{2,1,0:T(1,128)}), f32[32,1,128]{2,1,0:T(1,128)S(1)}, u32[]{:S(2)}, u32[]{:S(2)}) async-start(f32[32,1,128]{2,1,0:T(1,128)} %reshape.134), calls=%async_computation.3 | async-start | bytes 32768 | tf_op jit(solution)/shard_map/all_to_all | solution.py:116
  200.0 16.1 %all-to-all-start.4 = ((f32[32,1,128]{2,1,0:T(1,128)}), f32[32,1,128]{2,1,0:T(1,128)S(1)}, u32[]{:S(2)}, u32[]{:S(2)}) async-start(f32[32,1,128]{2,1,0:T(1,128)} %reshape.136), calls=%async_computation.4 | async-start | bytes 32768 | tf_op jit(solution)/shard_map/all_to_all | solution.py:117
  216.7 62.3 %all-to-all-start.2 = ((f32[32,8,2,8,128]{4,3,2,1,0:T(8,128)}), f32[32,8,2,8,128]{4,3,2,1,0:T(8,128)S(1)}, u32[]{:S(2)}, u32[]{:S(2)}) async-start(f32[32,8,2,8,128]{4,3,2,1,0:T(8,128)} %bitcast.186), calls=%async_computation.2 | async-start | bytes 4194304 | tf_op jit(solution)/shard_map/all_to_all | solution.py:115
  228.3 51.5 %copy-start.5 = (f32[8,2,8,128]{3,2,1,0:T(8,128)S(1)}, f32[8,2,8,128]{3,2,1,0:T(8,128)}, u32[]{:S(2)}) copy-start(f32[8,2,8,128]{3,2,1,0:T(8,128)} %reshape.123) | copy-start | bytes 196612
  327.3 92.7 %all-to-all-start.5 = ((bf16[4,2,2048]{2,1,0:T(2,128)(2,1)}), bf16[4,2,2048]{2,1,0:T(2,128)(2,1)}, u32[]{:S(2)}, u32[]{:S(2)}) async-start(bf16[4,2,2048]{2,1,0:T(2,128)(2,1)} %convert_element_type.60), calls=%async_computation.5 | async-start | bytes 65536 | tf_op jit(solution)/shard_map/all_to_all | solution.py:171
  331.2 2.8 copy-start.12
  331.2 6.2 %copy-start.8 = (f32[256,2,8]{0,2,1:T(8,128)}, f32[256,2,8]{0,2,1:T(8,128)S(1)}, u32[]{:S(2)}) copy-start(f32[256,2,8]{0,2,1:T(8,128)S(1)} %get-tuple-element.549) | copy-start | bytes 49156 | tf_op jit(solution)/shard_map/while
  341.0 2.4 copy-start
  344.5 2.8 copy-start.12
  344.5 6.2 %copy-start.8 = (f32[256,2,8]{0,2,1:T(8,128)}, f32[256,2,8]{0,2,1:T(8,128)S(1)}, u32[]{:S(2)}) copy-start(f32[256,2,8]{0,2,1:T(8,128)S(1)} %get-tuple-element.549) | copy-start | bytes 49156 | tf_op jit(solution)/shard_map/while
  359.3 2.8 copy-start.12
  359.3 6.2 %copy-start.8 = (f32[256,2,8]{0,2,1:T(8,128)}, f32[256,2,8]{0,2,1:T(8,128)S(1)}, u32[]{:S(2)}) copy-start(f32[256,2,8]{0,2,1:T(8,128)S(1)} %get-tuple-element.549) | copy-start | bytes 49156 | tf_op jit(solution)/shard_map/while
  370.6 2.4 copy-start
  374.1 2.8 copy-start.12
  374.1 6.2 %copy-start.8 = (f32[256,2,8]{0,2,1:T(8,128)}, f32[256,2,8]{0,2,1:T(8,128)S(1)}, u32[]{:S(2)}) copy-start(f32[256,2,8]{0,2,1:T(8,128)S(1)} %get-tuple-element.549) | copy-start | bytes 49156 | tf_op jit(solution)/shard_map/while
  388.9 2.8 copy-start.12
  388.9 6.2 %copy-start.8 = (f32[256,2,8]{0,2,1:T(8,128)}, f32[256,2,8]{0,2,1:T(8,128)S(1)}, u32[]{:S(2)}) copy-start(f32[256,2,8]{0,2,1:T(8,128)S(1)} %get-tuple-element.549) | copy-start | bytes 49156 | tf_op jit(solution)/shard_map/while
  403.8 2.8 copy-start.12
  403.8 6.2 %copy-start.8 = (f32[256,2,8]{0,2,1:T(8,128)}, f32[256,2,8]{0,2,1:T(8,128)S(1)}, u32[]{:S(2)}) copy-start(f32[256,2,8]{0,2,1:T(8,128)S(1)} %get-tuple-element.549) | copy-start | bytes 49156 | tf_op jit(solution)/shard_map/while
  420.1 5.8 %copy-start.1 = (f32[256,2,8,128]{0,3,2,1:T(8,128)S(1)}, f32[256,2,8,128]{0,3,2,1:T(8,128)}, u32[]{:S(2)}) copy-start(f32[256,2,8,128]{0,3,2,1:T(8,128)} %get-tuple-element.120) | copy-start | bytes 6291460
  421.4 25.9 %all-to-all-start.8 = ((bf16[4,768,256]{2,1,0:T(8,128)(2,1)}), bf16[4,768,256]{2,1,0:T(8,128)(2,1)}, u32[]{:S(2)}, u32[]{:S(2)}) async-start(bf16[4,768,256]{2,1,0:T(8,128)(2,1)} %broadcast_in_dim.79), calls=%async_computation.8 | async-start | bytes 3145728 | tf_op jit(solution)/shard_map/all_to_all | solution.py:24
  447.3 45.6 %all-to-all-start.6 = ((bf16[32,8,2,8,128]{4,3,2,1,0:T(8,128)(2,1)}), bf16[32,8,2,8,128]{4,3,2,1,0:T(8,128)(2,1)S(1)}, u32[]{:S(2)}, u32[]{:S(2)}) async-start(bf16[32,8,2,8,128]{4,3,2,1,0:T(8,128)(2,1)} %bitcast.10), calls=%async_computation.6 | async-start | bytes 2097152 | tf_op jit(solution)/shard_map/all_to_all | solution.py:41
  494.1 23.1 %all-to-all-start.9 = ((bf16[4,768,256]{2,1,0:T(8,128)(2,1)}), bf16[4,768,256]{2,1,0:T(8,128)(2,1)S(1)}, u32[]{:S(2)}, u32[]{:S(2)}) async-start(bf16[4,768,256]{2,1,0:T(8,128)(2,1)} %broadcast_in_dim.80), calls=%async_computation.9 | async-start | bytes 3145728 | tf_op jit(solution)/shard_map/all_to_all | solution.py:24
  517.2 10.5 %all-to-all-start.7 = ((bf16[4,2,2048]{2,1,0:T(2,128)(2,1)}), bf16[4,2,2048]{2,1,0:T(2,128)(2,1)S(1)}, u32[]{:S(2)}, u32[]{:S(2)}) async-start(bf16[4,2,2048]{2,1,0:T(2,128)(2,1)} %convert_element_type.64), calls=%async_computation.7 | async-start | bytes 65536 | tf_op jit(solution)/shard_map/all_to_all | solution.py:172
  (17 other events, 23.3 us)
Sparse Core Ops, SparseCore 0:
  29.9 95.0 all-gather.1
where the time goes:
time: 540 us; the launch traced here: 537 us
  waiting for transfers between devices  238 us (44%)
  matrix products  92 us (17%)
  blocking collectives  59.2 us (11%)
  local copies, waits for them, and re-layouts  48.3 us (9%)
  starting transfers between devices  48.2 us (9%)
  loops' own time  24.8 us (5%)
  between operations  14.4 us (3%)
  other arithmetic  11.2 us (2%)
    all_gather x1, waiting for transfers between devices, in_one_piece(): result, at, outs = (lax.all_gather(both, axis, axis=dim, tiled=True), 0, [])  93 us
    all_to_all x1, waiting for transfers between devices, per_device(): lax.all_to_all(sent[0], 'mem', split_axis=0, concat_axis=0, tiled=True)  50.4 us
    all_gather x1, blocking collectives, in_one_piece(): result, at, outs = (lax.all_gather(both, axis, axis=dim, tiled=True), 0, [])  46.2 us
    all_to_all x2, waiting for transfers between devices, sent_to_all(): lax.all_to_all(jnp.broadcast_to(array[None], (count, *array.shape)), axis...  38.3 us
    all_to_all x1, waiting for transfers between devices, sent_and_summed(): lax.all_to_all(pieces, axis, split_axis=0, concat_axis=0, tiled=True)  31.6 us
    dot_general x12, matrix products, frame_scores(): jnp.einsum('rghd,jgd->rghj', query_four, key_block, preferred_element_typ...  21.3 us
    dot_general x6, matrix products, forward_step(): jnp.einsum('rghj,jgd->rghd', weight.astype(jnp.bfloat16), value_block, pr...  20.9 us
    dot_general x6, matrix products, backward_step(): jnp.einsum('rghj,jgd->rghd', score_grad, key_block, preferred_element_typ...  19.1 us
  transfers between devices with their start and end apart: 10, of which 9 were waited for; matrix products, arithmetic and copies ran while one was open for 18% of the time, Pallas kernels for 0%

commit v1 on v0

--- a/solution.py
+++ b/solution.py
@@ -54,7 +54,12 @@
     mem_count = lax.axis_size("mem")
     local_query, local_grad = (
         lax.all_to_all(queries, "kvh", split_axis=1, concat_axis=0, tiled=True),
-        lax.all_to_all(output_gradient, "kvh", split_axis=1, concat_axis=0, tiled=True),
+        jnp.concatenate(
+            lax.all_to_all(
+                jnp.stack(jnp.split(output_gradient, lax.axis_size("kvh"), axis=1)), "kvh", 0, 0
+            ),
+            axis=0,
+        ),
     )
     query_rows, grad_rows = in_one_piece((local_query, local_grad), "mem", 0, 1)
     group_size = query_rows.shape[0]

time: 540 us -> 540 us (level)
  blocking collectives: 59.2 us -> 46.2 us
  starting transfers between devices: 48.2 us -> 55.6 us
    all_to_all x1 -> x0, blocking collectives: 13.1 us -> none  [per_device(): lax.all_to_all(output_gradient, 'kvh', split_axis=1, concat_axis=0, tiled...]
    all_to_all x0 -> x1, waiting for transfers between devices: none -> 5.55 us  [per_device(): lax.all_to_all(jnp.stack(jnp.split(output_gradient, lax.axis_size('kvh'),...]
  transfers between devices with their start and end apart: 10 -> 11, of which waited for: 9 -> 10; matrix products, arithmetic and copies ran while one was open for 18% -> 18% of each run, Pallas kernels for 0% -> 0%
where the time goes in v1:
time: 540 us; the launch traced here: 537 us
  waiting for transfers between devices  243 us (45%)
  matrix products  92 us (17%)
  starting transfers between devices  55.6 us (10%)
  local copies, waits for them, and re-layouts  49.1 us (9%)
  blocking collectives  46.2 us (9%)
  loops' own time  24.8 us (5%)
  between operations  14.4 us (3%)
  other arithmetic  11.9 us (2%)
    all_gather x1, waiting for transfers between devices, in_one_piece(): result, at, outs = (lax.all_gather(both, axis, axis=dim, tiled=True), 0, [])  93 us
    all_to_all x1, waiting for transfers between devices, per_device(): lax.all_to_all(sent[0], 'mem', split_axis=0, concat_axis=0, tiled=True)  50.5 us
    all_gather x1, blocking collectives, in_one_piece(): result, at, outs = (lax.all_gather(both, axis, axis=dim, tiled=True), 0, [])  46.2 us
    all_to_all x2, waiting for transfers between devices, sent_to_all(): lax.all_to_all(jnp.broadcast_to(array[None], (count, *array.shape)), axis...  38.3 us
    all_to_all x1, waiting for transfers between devices, sent_and_summed(): lax.all_to_all(pieces, axis, split_axis=0, concat_axis=0, tiled=True)  31.6 us
    dot_general x12, matrix products, frame_scores(): jnp.einsum('rghd,jgd->rghj', query_four, key_block, preferred_element_typ...  21.3 us
    dot_general x6, matrix products, forward_step(): jnp.einsum('rghj,jgd->rghd', weight.astype(jnp.bfloat16), value_block, pr...  20.9 us
    dot_general x6, matrix products, backward_step(): jnp.einsum('rghj,jgd->rghd', score_grad, key_block, preferred_element_typ...  19.1 us
  transfers between devices with their start and end apart: 11, of which 10 were waited for; matrix products, arithmetic and copies ran while one was open for 18% of the time, Pallas kernels for 0%

profile of v1, /device:TPU:8, one launch (start us, length us, event | category | flops | bytes accessed | tf_op | source)
XLA Modules:
  0.0 536.6 jit_solution(8106337823995075407)
XLA Ops:
  7.2 7.4 %all-to-all-start = ((bf16[2,4,2048]{2,0,1:T(2,128)(2,1)}), bf16[2,4,2048]{2,0,1:T(2,128)(2,1)S(1)}, u32[]{:S(2)}, u32[]{:S(2)}) async-start(bf16[2,4,2048]{2,0,1:T(2,128)(2,1)} %bitcast.202), calls=%async_computation | async-start | bytes 65536 | tf_op jit(solution)/shard_map/all_to_all | solution.py:56
  16.0 4.2 all-to-all-done
  20.3 3.3 all-to-all-start.1
  23.6 5.5 %all-to-all-done.1 = bf16[4,2,2048]{2,1,0:T(2,128)(2,1)S(1)} async-done(((bf16[4,2,2048]{2,1,0:T(2,128)(2,1)}), bf16[4,2,2048]{2,1,0:T(2,128)(2,1)S(1)}, u32[]{:S(2)}, u32[]{:S(2)}) %all-to-all-start.1) | async-done | bytes 32800 | tf_op jit(solution)/shard_map/all_to_all | solution.py:58
  32.0 93.0 %all-gather.2.cloned.1.call-done = bf16[256,4096]{1,0:T(8,128)(2,1)} async-done(((bf16[8,4096]{1,0:T(8,128)(2,1)}), bf16[256,4096]{1,0:T(8,128)(2,1)}) %all-gather.2.cloned.1.call-update) | async-done | bytes 2097168 | tf_op jit(solution)/shard_map/all_gather | solution.py:15
  129.6 50.9 %while.30 = (s32[]{:T(128)}, f32[256,2,8]{0,2,1:T(8,128)S(1)}, f32[256,2,8]{0,2,1:T(8,128)S(1)}, f32[256,2,8,128]{0,3,2,1:T(8,128)}, s32[6]{0:T(128)S(1)}, /*ind...) while((s32[]{:T(128)}, f32[256,2,8]{0,2,1:T(8,128)S(1)}, ...), condition=%wide.region_5.6_spmd.clone, body=%wide.region_2.5_spmd.clone.sunk | while | flops 276844544 | bytes 12191419 | solution.py:110
  141.8 3.7 bitcast_add_fusion.4
  150.6 3.7 bitcast_add_fusion.4
  159.3 3.7 bitcast_add_fusion.4
  168.1 3.7 bitcast_add_fusion.4
  176.8 3.7 bitcast_add_fusion.4
  183.3 5.6 %all-to-all-start.3 = ((f32[32,1,128]{2,1,0:T(1,128)}), f32[32,1,128]{2,1,0:T(1,128)S(1)}, u32[]{:S(2)}, u32[]{:S(2)}) async-start(f32[32,1,128]{2,1,0:T(1,128)} %reshape.133), calls=%async_computation.3 | async-start | bytes 32768 | tf_op jit(solution)/shard_map/all_to_all | solution.py:121
  191.7 8.3 %all-to-all-done.3 = f32[32,1,128]{2,1,0:T(1,128)S(1)} async-done(((f32[32,1,128]{2,1,0:T(1,128)}), f32[32,1,128]{2,1,0:T(1,128)S(1)}, u32[]{:S(2)}, u32[]{:S(2)}) %all-to-all-start.3) | async-done | bytes 16416 | tf_op jit(solution)/shard_map/all_to_all | solution.py:121
  200.0 4.9 all-to-all-start.4
  206.9 9.2 %all-to-all-done.4 = f32[32,1,128]{2,1,0:T(1,128)S(1)} async-done(((f32[32,1,128]{2,1,0:T(1,128)}), f32[32,1,128]{2,1,0:T(1,128)S(1)}, u32[]{:S(2)}, u32[]{:S(2)}) %all-to-all-start.4) | async-done | bytes 16416 | tf_op jit(solution)/shard_map/all_to_all | solution.py:122
  216.7 5.1 all-to-all-start.2
  228.6 50.5 %all-to-all-done.2 = f32[32,8,2,8,128]{4,3,2,1,0:T(8,128)S(1)} async-done(((f32[32,8,2,8,128]{4,3,2,1,0:T(8,128)}), f32[32,8,2,8,128]{4,3,2,1,0:T(8,128)S(1)}, u32[]{:S(2)}, u32[]{:S(2)}) %all-to-all-start.2) | async-done | bytes 2097184 | tf_op jit(solution)/shard_map/all_to_all | solution.py:120
  280.1 46.2 %all_gather.7 = f32[256,4,8]{2,1,0:T(4,128)S(1)} all-gather(f32[8,4,8]{2,1,0:T(4,128)S(1)} %copy.126), channel_id=1, replica_groups=mesh['mem'=32,'kvh'=4,'row'=4] {'mem'}, dimensions={0}, use_global_device_ids=true | all-gather | bytes 33792 | tf_op jit(solution)/shard_map/all_gather | solution.py:15
  327.3 3.9 all-to-all-start.5
  331.2 87.4 %while.31 = (s32[]{:T(128)}, f32[256,2,8,128]{0,3,2,1:T(8,128)}, bf16[6,128,2,128]{3,1,2,0:T(8,128)(2,1)}, bf16[6,128,2,128]{3,1,2,0:T(8,128)(2,1)}, s32[6]{0:T(...) while((s32[]{:T(128)}, f32[256,2,8,128]{0,3,2,1:T(8,128)}, ...), condition=%wide.region_11.12_spmd.clone, body=%wide.region_10.11_spmd.clone.sunk | while | flops 676888576 | bytes 22776864 | solution.py:162
  352.4 3.4 bitcast_add_fusion.5
  367.2 3.4 bitcast_add_fusion.5
  382.0 3.4 bitcast_add_fusion.5
  396.8 3.4 bitcast_add_fusion.5
  411.7 3.4 bitcast_add_fusion.5
  421.4 4.5 all-to-all-start.8
  427.8 19.5 %all-to-all-done.8 = bf16[4,768,256]{2,1,0:T(8,128)(2,1)} async-done(((bf16[4,768,256]{2,1,0:T(8,128)(2,1)}), bf16[4,768,256]{2,1,0:T(8,128)(2,1)}, u32[]{:S(2)}, u32[]{:S(2)}) %all-to-all-start.8) | async-done | bytes 1572896 | tf_op jit(solution)/shard_map/all_to_all | solution.py:24
  447.3 12.5 %all-to-all-start.6 = ((bf16[32,8,2,8,128]{4,3,2,1,0:T(8,128)(2,1)}), bf16[32,8,2,8,128]{4,3,2,1,0:T(8,128)(2,1)S(1)}, u32[]{:S(2)}, u32[]{:S(2)}) async-start(bf16[32,8,2,8,128]{4,3,2,1,0:T(8,128)(2,1)} %bitcast.12), calls=%async_computation.6 | async-start | bytes 2097152 | tf_op jit(solution)/shard_map/all_to_all | solution.py:41
  461.2 31.6 %all-to-all-done.6 = bf16[32,8,2,8,128]{4,3,2,1,0:T(8,128)(2,1)S(1)} async-done(((bf16[32,8,2,8,128]{4,3,2,1,0:T(8,128)(2,1)}), bf16[32,8,2,8,128]{4,3,2,1,0:T(8,128)(2,1)S(1)}, u32[]{:S(2)}, u32[]{:S(2)}) %all-to-all-start.6) | async-done | bytes 1048608 | tf_op jit(solution)/shard_map/all_to_all | solution.py:41
  494.1 3.6 all-to-all-start.9
  498.5 18.8 %all-to-all-done.9 = bf16[4,768,256]{2,1,0:T(8,128)(2,1)S(1)} async-done(((bf16[4,768,256]{2,1,0:T(8,128)(2,1)}), bf16[4,768,256]{2,1,0:T(8,128)(2,1)S(1)}, u32[]{:S(2)}, u32[]{:S(2)}) %all-to-all-start.9) | async-done | bytes 1572896 | tf_op jit(solution)/shard_map/all_to_all | solution.py:24
  517.2 4.8 all-to-all-start.7
  (249 shorter events, 119.1 us)
Async XLA Ops:
  7.2 23.9 %copy-start.4 = (bf16[768,256]{1,0:T(8,128)(2,1)S(1)}, bf16[768,256]{1,0:T(8,128)(2,1)}, u32[]{:S(2)}) copy-start(bf16[768,256]{1,0:T(8,128)(2,1)} %param.13) | copy-start | bytes 1179652
  7.2 24.0 %copy-start.11 = (s32[96]{0:T(128)S(1)}, s32[96]{0:T(128)}, u32[]{:S(2)}) copy-start(s32[96]{0:T(128)} %param.15) | copy-start | bytes 1156
  7.2 24.3 %copy-start.10 = (s32[128,2]{0,1:T(2,128)S(1)}, s32[128,2]{0,1:T(2,128)}, u32[]{:S(2)}) copy-start(s32[128,2]{0,1:T(2,128)} %param.14) | copy-start | bytes 3076
  7.2 13.1 %all-to-all-start = ((bf16[2,4,2048]{2,0,1:T(2,128)(2,1)}), bf16[2,4,2048]{2,0,1:T(2,128)(2,1)S(1)}, u32[]{:S(2)}, u32[]{:S(2)}) async-start(bf16[2,4,2048]{2,0,1:T(2,128)(2,1)} %bitcast.202), calls=%async_computation | async-start | bytes 65536 | tf_op jit(solution)/shard_map/all_to_all | solution.py:56
  20.3 8.9 %all-to-all-start.1 = ((bf16[4,2,2048]{2,1,0:T(2,128)(2,1)}), bf16[4,2,2048]{2,1,0:T(2,128)(2,1)S(1)}, u32[]{:S(2)}, u32[]{:S(2)}) async-start(bf16[4,2,2048]{2,1,0:T(2,128)(2,1)} %pad_maximum_fusion.1), calls=%async_computation.1 | async-start | bytes 65536 | tf_op jit(solution)/shard_map/all_to_all | solution.py:58
  23.5 101.5 %all-gather.2.cloned.1.call-start = ((), (), s32[]{:S(2)}) async-start(), calls=%async_computation.10 | async-start | bytes 2162688 | tf_op jit(solution)/shard_map/all_gather | solution.py:15
  180.6 26.4 %copy-start.3 = (bf16[6,128,2,128]{3,2,1,0:T(2,128)(2,1)}, bf16[6,128,2,128]{3,2,1,0:T(2,128)(2,1)S(1)}, u32[]{:S(2)}) copy-start(bf16[6,128,2,128]{3,2,1,0:T(2,128)(2,1)S(1)} %get-tuple-element.598) | copy-start | bytes 1179652
  180.6 26.4 %copy-start.6 = (pred[256,6]{0,1:T(8,128)(4,1)}, pred[256,6]{0,1:T(8,128)(4,1)S(1)}, u32[]{:S(2)}) copy-start(pred[256,6]{0,1:T(8,128)(4,1)S(1)} %get-tuple-element.605) | copy-start | bytes 4612
  180.6 24.4 %copy-start.2 = (f32[256,2,8,128]{0,3,2,1:T(8,128)S(1)}, f32[256,2,8,128]{0,3,2,1:T(8,128)}, u32[]{:S(2)}) copy-start(f32[256,2,8,128]{0,3,2,1:T(8,128)} %get-tuple-element.117) | copy-start | bytes 6291460
  183.3 16.7 %all-to-all-start.3 = ((f32[32,1,128]{2,1,0:T(1,128)}), f32[32,1,128]{2,1,0:T(1,128)S(1)}, u32[]{:S(2)}, u32[]{:S(2)}) async-start(f32[32,1,128]{2,1,0:T(1,128)} %reshape.133), calls=%async_computation.3 | async-start | bytes 32768 | tf_op jit(solution)/shard_map/all_to_all | solution.py:121
  200.0 16.1 %all-to-all-start.4 = ((f32[32,1,128]{2,1,0:T(1,128)}), f32[32,1,128]{2,1,0:T(1,128)S(1)}, u32[]{:S(2)}, u32[]{:S(2)}) async-start(f32[32,1,128]{2,1,0:T(1,128)} %reshape.135), calls=%async_computation.4 | async-start | bytes 32768 | tf_op jit(solution)/shard_map/all_to_all | solution.py:122
  216.7 62.3 %all-to-all-start.2 = ((f32[32,8,2,8,128]{4,3,2,1,0:T(8,128)}), f32[32,8,2,8,128]{4,3,2,1,0:T(8,128)S(1)}, u32[]{:S(2)}, u32[]{:S(2)}) async-start(f32[32,8,2,8,128]{4,3,2,1,0:T(8,128)} %bitcast.191), calls=%async_computation.2 | async-start | bytes 4194304 | tf_op jit(solution)/shard_map/all_to_all | solution.py:120
  228.2 51.5 %copy-start.5 = (f32[8,2,8,128]{3,2,1,0:T(8,128)S(1)}, f32[8,2,8,128]{3,2,1,0:T(8,128)}, u32[]{:S(2)}) copy-start(f32[8,2,8,128]{3,2,1,0:T(8,128)} %reshape.122) | copy-start | bytes 196612
  327.3 92.8 %all-to-all-start.5 = ((bf16[4,2,2048]{2,1,0:T(2,128)(2,1)}), bf16[4,2,2048]{2,1,0:T(2,128)(2,1)}, u32[]{:S(2)}, u32[]{:S(2)}) async-start(bf16[4,2,2048]{2,1,0:T(2,128)(2,1)} %convert_element_type.60), calls=%async_computation.5 | async-start | bytes 65536 | tf_op jit(solution)/shard_map/all_to_all | solution.py:176
  331.2 2.8 copy-start.12
  331.2 6.2 %copy-start.8 = (f32[256,2,8]{0,2,1:T(8,128)}, f32[256,2,8]{0,2,1:T(8,128)S(1)}, u32[]{:S(2)}) copy-start(f32[256,2,8]{0,2,1:T(8,128)S(1)} %get-tuple-element.574) | copy-start | bytes 49156 | tf_op jit(solution)/shard_map/while
  341.0 2.4 copy-start
  344.5 2.8 copy-start.12
  344.5 6.2 %copy-start.8 = (f32[256,2,8]{0,2,1:T(8,128)}, f32[256,2,8]{0,2,1:T(8,128)S(1)}, u32[]{:S(2)}) copy-start(f32[256,2,8]{0,2,1:T(8,128)S(1)} %get-tuple-element.574) | copy-start | bytes 49156 | tf_op jit(solution)/shard_map/while
  359.3 2.8 copy-start.12
  359.3 6.2 %copy-start.8 = (f32[256,2,8]{0,2,1:T(8,128)}, f32[256,2,8]{0,2,1:T(8,128)S(1)}, u32[]{:S(2)}) copy-start(f32[256,2,8]{0,2,1:T(8,128)S(1)} %get-tuple-element.574) | copy-start | bytes 49156 | tf_op jit(solution)/shard_map/while
  374.1 2.8 copy-start.12
  374.1 6.2 %copy-start.8 = (f32[256,2,8]{0,2,1:T(8,128)}, f32[256,2,8]{0,2,1:T(8,128)S(1)}, u32[]{:S(2)}) copy-start(f32[256,2,8]{0,2,1:T(8,128)S(1)} %get-tuple-element.574) | copy-start | bytes 49156 | tf_op jit(solution)/shard_map/while
  388.9 2.8 copy-start.12
  388.9 6.2 %copy-start.8 = (f32[256,2,8]{0,2,1:T(8,128)}, f32[256,2,8]{0,2,1:T(8,128)S(1)}, u32[]{:S(2)}) copy-start(f32[256,2,8]{0,2,1:T(8,128)S(1)} %get-tuple-element.574) | copy-start | bytes 49156 | tf_op jit(solution)/shard_map/while
  403.8 2.8 copy-start.12
  403.8 6.2 %copy-start.8 = (f32[256,2,8]{0,2,1:T(8,128)}, f32[256,2,8]{0,2,1:T(8,128)S(1)}, u32[]{:S(2)}) copy-start(f32[256,2,8]{0,2,1:T(8,128)S(1)} %get-tuple-element.574) | copy-start | bytes 49156 | tf_op jit(solution)/shard_map/while
  420.1 5.8 %copy-start.1 = (f32[256,2,8,128]{0,3,2,1:T(8,128)S(1)}, f32[256,2,8,128]{0,3,2,1:T(8,128)}, u32[]{:S(2)}) copy-start(f32[256,2,8,128]{0,3,2,1:T(8,128)} %get-tuple-element.120) | copy-start | bytes 6291460
  421.4 25.9 %all-to-all-start.8 = ((bf16[4,768,256]{2,1,0:T(8,128)(2,1)}), bf16[4,768,256]{2,1,0:T(8,128)(2,1)}, u32[]{:S(2)}, u32[]{:S(2)}) async-start(bf16[4,768,256]{2,1,0:T(8,128)(2,1)} %broadcast_in_dim.79), calls=%async_computation.8 | async-start | bytes 3145728 | tf_op jit(solution)/shard_map/all_to_all | solution.py:24
  447.3 45.6 %all-to-all-start.6 = ((bf16[32,8,2,8,128]{4,3,2,1,0:T(8,128)(2,1)}), bf16[32,8,2,8,128]{4,3,2,1,0:T(8,128)(2,1)S(1)}, u32[]{:S(2)}, u32[]{:S(2)}) async-start(bf16[32,8,2,8,128]{4,3,2,1,0:T(8,128)(2,1)} %bitcast.12), calls=%async_computation.6 | async-start | bytes 2097152 | tf_op jit(solution)/shard_map/all_to_all | solution.py:41
  494.1 23.1 %all-to-all-start.9 = ((bf16[4,768,256]{2,1,0:T(8,128)(2,1)}), bf16[4,768,256]{2,1,0:T(8,128)(2,1)S(1)}, u32[]{:S(2)}, u32[]{:S(2)}) async-start(bf16[4,768,256]{2,1,0:T(8,128)(2,1)} %broadcast_in_dim.80), calls=%async_computation.9 | async-start | bytes 3145728 | tf_op jit(solution)/shard_map/all_to_all | solution.py:24
  517.2 10.5 %all-to-all-start.7 = ((bf16[4,2,2048]{2,1,0:T(2,128)(2,1)}), bf16[4,2,2048]{2,1,0:T(2,128)(2,1)S(1)}, u32[]{:S(2)}, u32[]{:S(2)}) async-start(bf16[4,2,2048]{2,1,0:T(2,128)(2,1)} %convert_element_type.64), calls=%async_computation.7 | async-start | bytes 65536 | tf_op jit(solution)/shard_map/all_to_all | solution.py:177
  (18 other events, 25.6 us)
Sparse Core Ops, SparseCore 0:
  29.9 95.0 all-gather.1
